TPU v7x, 256 devices: a whole 4x4x8 slice. The times are simulated.
256 devices in a mesh: vox: 128 (over x, z, y), sub: 2 (over core).
Axes of the slice: x: 4, y: 4, z: 8, core: 2. Of those that a mesh axis runs over, the one named last changes fastest.
Arguments:
- movie: bfloat16 [262144, 4096], P(('vox', 'sub')), may hold values from -120 to 120
- test_matrix: bfloat16 [4096, 256], replicated, may hold values from -0.09375 to 0.09375
Outputs:
- basis: float32 [262144, 256], P(('vox', 'sub'))
- r_factor: float32 [256, 256], replicated
- projected: float32 [256, 4096], P(None, ('vox', 'sub'))
All inputs are finite; a program needn't handle non-finite values.
Results may differ from a plain program's by a relative error of at most 0.00063.
Values sent between devices are 32-bit elements; how exact they have to be, the bound alone decides.
A program may use at most 128 MiB of HBM per device.

v0:
```python
import jax
import jax.numpy as jnp
from jax import lax
from jax.sharding import PartitionSpec as P


def square_sum(matrix):
    return jnp.dot(matrix.T, matrix, precision=lax.Precision.HIGHEST)


def local(movie, test_matrix):
    sketch = jnp.dot(movie, test_matrix, preferred_element_type=jnp.float32)
    devices_all = lax.axis_size(("vox", "sub"))
    sketch_b = sketch.astype(jnp.bfloat16)
    partial_sum = lax.dot_general(
        sketch_b, movie, (((0,), (0,)), ((), ())), preferred_element_type=jnp.float32
    )
    columns = movie.shape[1] // devices_all
    total = lax.psum(partial_sum, ("vox", "sub"))
    mine = lax.dynamic_slice_in_dim(total, lax.axis_index(("vox", "sub")) * columns, columns, 1)
    gram = lax.psum(square_sum(sketch), ("vox", "sub"))
    lower = jnp.linalg.cholesky(gram)
    width = sketch.shape[1]
    identity = jnp.eye(width, dtype=jnp.float32)
    inverse = lax.linalg.triangular_solve(lower, identity, left_side=True, lower=True)
    scale = jnp.sqrt(jnp.float32(sketch.shape[0] * devices_all))
    basis = jnp.dot(sketch, inverse.T, precision=lax.Precision.HIGHEST) * scale
    projected = jnp.dot(inverse, mine, precision=lax.Precision.HIGHEST)
    return (basis, lower.T / scale, projected)


def solution(mesh):
    placed = (P(("vox", "sub"), None), P())
    return jax.shard_map(
        local,
        mesh=mesh,
        in_specs=placed,
        out_specs=(P(("vox", "sub"), None), P(), P(None, ("vox", "sub"))),
        check_vma=False,
    )
```

profile of v0, /device:TPU:2, one launch (start us, length us, event | category | flops | bytes accessed | tf_op | source)
XLA Modules:
  0.0 380.6 jit_solution(14960276804258986143)
XLA Ops:
  7.2 0.0 copy-start
  7.2 0.0 all-reduce.4.cloned.1.call-start
  7.2 1.5 copy-done
  8.8 0.0 copy-start.1
  8.8 5.9 %fusion.17 = f32[1024,256]{1,0:T(8,128)S(1)} fusion(bf16[1024,4096]{1,0:T(8,128)(2,1)} %param.2, bf16[4096,256]{1,0:T(8,128)(2,1)S(1)} %copy-done), kind=kOutput, calls=%fused_computation.40 | convolution fusion | flops 2147483648 | bytes 11534336 | tf_op jit(solution)/shard_map/dot_general | solution.py:12
  14.6 0.0 copy-done.1
  14.6 4.3 %fusion = f32[256,4096]{1,0:T(8,128)} fusion(bf16[1024,4096]{1,0:T(8,128)(2,1)S(1)} %copy-done.1, f32[1024,256]{1,0:T(8,128)S(1)} %fusion.17), kind=kOutput, calls=%fused_computation.5 | convolution fusion | flops 2147745792 | bytes 13631488 | tf_op jit(solution)/shard_map/dot_general | solution.py:15
  19.0 2.5 fusion.18
  21.5 0.0 all-reduce.4.cloned.1.call-update
  21.6 0.6 iota_compare_fusion
  22.2 274.1 %all-reduce.4.cloned.1.call-done = (f32[256,256]{0,1:T(8,128)}, f32[256,4096]{1,0:T(8,128)}) async-done(((f32[256,256]{0,1:T(8,128)}, f32[256,4096]{1,0:T(8,128)}), (f32[256,256]{0,1:T(8,128)}, f32[256,4096]{1,0:T(8,128)})) %all-reduce.4.cloned.1.call-update) | async-done | bytes 4456464 | tf_op jit(solution)/shard_map/psum | solution.py:21
  296.3 1.1 copy.6
  297.3 1.0 fusion.2
  298.3 0.0 copy-start.3
  298.3 0.7 copy-done.3
  299.0 11.7 %cholesky.50 = f32[128,128]{1,0:T(8,128)S(1)} custom-call(f32[128,128]{1,0:T(8,128)S(1)} %cholesky.118), custom_call_target="Cholesky" | custom-call | tf_op jit(solution)/shard_map/jit(cholesky)/cholesky | solution.py:22
  310.8 9.8 %custom-call.14 = f32[1,128,128]{1,2,0:T(8,128)S(1)} custom-call(f32[1,128,128]{2,1,0:T(8,128)S(1)} %get-tuple-element.31), custom_call_target="InvertDiagBlocksLowerTriangular" | custom-call | tf_op jit(solution)/shard_map/jit(cholesky)/cholesky | solution.py:22
  320.6 0.2 cholesky.113
  320.8 1.0 constant_dynamic-update-slice_fusion
  321.9 1.1 convolution_subtract_fusion.1
  323.0 11.7 %cholesky.105 = f32[128,128]{1,0:T(8,128)S(1)} custom-call(f32[128,128]{1,0:T(8,128)S(1)} %convolution_subtract_fusion.1), custom_call_target="Cholesky" | custom-call | tf_op jit(solution)/shard_map/jit(cholesky)/cholesky | solution.py:22
  334.7 0.0 copy-start.2
  334.7 0.7 compare_reduce_fusion
  336.7 0.0 copy-done.2
  336.7 1.7 multiply_bitcast_fusion
  338.4 0.1 triangular_solve.63
  338.5 5.2 %while.1 = (s32[]{:T(128)}, f32[256,256]{1,0:T(8,128)S(1)}, s32[2,2]{1,0:T(2,128)S(1)}, f32[2,128,128]{2,1,0:T(8,128)}, s32[]{:T(128)}) while((s32[]{:T(128)}, f32[256,256]{1,0:T(8,128)S(1)}, s32[2,2]{1,0:T(2,128)S(1)}, f32[2,128,128]{2,1,0:T(8,128)}, s32[]{:T(128)}) %tuple.29), condition=%wide.while_cond, body=%wide.while_body.sunk | while | flops 2 | bytes 132705 | solution.py:25
  338.5 0.6 fusion.30
  339.1 2.0 bitcast_dynamic-update-slice_fusion.2
  341.1 0.6 fusion.30
  341.7 2.0 bitcast_dynamic-update-slice_fusion.2
  343.7 21.1 %custom-call.15 = f32[2,128,128]{1,2,0:T(8,128)} custom-call(f32[2,128,128]{2,1,0:T(8,128)} %get-tuple-element.10), custom_call_target="InvertDiagBlocksLowerTriangular" | custom-call | tf_op jit(solution)/shard_map/triangular_solve | solution.py:25
  364.8 1.1 fusion.6
  365.9 1.0 convolution_subtract_fusion
  366.9 1.2 fusion.9
  368.1 2.0 convolution_multiply_fusion
  370.1 1.8 copy.7
  371.8 1.9 fusion.4
  (7 shorter events, 0.1 us)
Async XLA Ops:
  7.2 1.6 copy-start
  7.2 289.1 %all-reduce.4.cloned.1.call-start = ((), (), s32[]{:S(2)}) async-start(), calls=%async_computation | async-start | bytes 8912896 | tf_op jit(solution)/shard_map/psum | solution.py:21
  8.8 5.9 %copy-start.1 = (bf16[1024,4096]{1,0:T(8,128)(2,1)S(1)}, bf16[1024,4096]{1,0:T(8,128)(2,1)}, u32[]{:S(2)}) copy-start(bf16[1024,4096]{1,0:T(8,128)(2,1)} %param.2) | copy-start | bytes 25165828
  298.3 0.7 copy-start.3
  334.7 2.0 copy-start.2
Sparse Core Ops, SparseCore 0:
  21.7 274.5 all-reduce.3
where the time goes:
time: 381 us
  waiting for transfers between devices  274 us (72%)
  other arithmetic  58.5 us (15%)
  matrix products  22.1 us (6%)
  between operations  15.4 us (4%)
  local copies, waits for them, and re-layouts  10.6 us (3%)
    psum x1, waiting for transfers between devices, local(): gram = lax.psum(square_sum(sketch), ('vox', 'sub'))  274 us
    another operation x6, other arithmetic, local(): lower = jnp.linalg.cholesky(gram)  34 us
    another operation x2, other arithmetic, local(): lax.linalg.triangular_solve(lower, identity, left_side=True, lower=True)  21.1 us
  transfers between devices with their start and end apart: 1, of which 1 were waited for; matrix products, arithmetic and copies ran while one was open for 0% of the time, Pallas kernels for 0%

commit v1 on v0

--- a/solution.py
+++ b/solution.py
@@ -18,7 +18,7 @@
     columns = movie.shape[1] // devices_all
     total = lax.psum(partial_sum, ("vox", "sub"))
     mine = lax.dynamic_slice_in_dim(total, lax.axis_index(("vox", "sub")) * columns, columns, 1)
-    gram = lax.psum(square_sum(sketch), ("vox", "sub"))
+    gram = lax.psum(lax.psum(square_sum(sketch), "vox"), "sub")
     lower = jnp.linalg.cholesky(gram)
     width = sketch.shape[1]
     identity = jnp.eye(width, dtype=jnp.float32)

time: 381 us -> 552 us (1.45)
  waiting for transfers between devices: 274 us -> 442 us
    psum x1 -> x3, waiting for transfers between devices: 274 us -> 442 us  [the longest x2 239 us: local(): gram = lax.psum(lax.psum(square_sum(sketch), 'vox'), 'sub')]
  transfers between devices with their start and end apart: 1 -> 3, of which waited for: 1 -> 3; matrix products, arithmetic and copies ran while one was open for 0% -> 15% of each run, Pallas kernels for 0% -> 0%
where the time goes in v1:
time: 552 us; the launch traced here: 551 us
  waiting for transfers between devices  442 us (80%)
  other arithmetic  58.5 us (11%)
  matrix products  25.3 us (5%)
  between operations  15.1 us (3%)
  local copies, waits for them, and re-layouts  10.2 us (2%)
    psum x2, waiting for transfers between devices, local(): gram = lax.psum(lax.psum(square_sum(sketch), 'vox'), 'sub')  239 us
    psum x1, waiting for transfers between devices, local(): total = lax.psum(partial_sum, ('vox', 'sub'))  202 us
    another operation x6, other arithmetic, local(): lower = jnp.linalg.cholesky(gram)  34.1 us
    another operation x2, other arithmetic, local(): lax.linalg.triangular_solve(lower, identity, left_side=True, lower=True)  21.1 us
  transfers between devices with their start and end apart: 3, of which 3 were waited for; matrix products, arithmetic and copies ran while one was open for 15% of the time, Pallas kernels for 0%

profile of v1, /device:TPU:2, one launch (start us, length us, event | category | flops | bytes accessed | tf_op | source)
XLA Modules:
  0.0 551.1 jit_solution(4584890378576869725)
XLA Ops:
  7.2 0.0 copy-start
  7.2 0.0 all-reduce.5.cloned.1.call-start
  7.2 1.5 copy-done
  8.8 5.7 %fusion.17 = f32[1024,256]{1,0:T(8,128)S(1)} fusion(bf16[1024,4096]{1,0:T(8,128)(2,1)} %param.2, bf16[4096,256]{1,0:T(8,128)(2,1)S(1)} %copy-done), kind=kOutput, calls=%fused_computation.40 | convolution fusion | flops 2147483648 | bytes 11534336 | tf_op jit(solution)/shard_map/dot_general | solution.py:12
  14.5 2.5 fusion.18
  17.0 0.0 all-reduce.5.cloned.1.call-update
  17.0 0.0 all-reduce.7.cloned.1.call-start
  17.1 218.7 %all-reduce.5.cloned.1.call-done = f32[256,256]{0,1:T(8,128)} async-done(((f32[256,256]{0,1:T(8,128)}), f32[256,256]{0,1:T(8,128)}) %all-reduce.5.cloned.1.call-update) | async-done | bytes 262160 | tf_op jit(solution)/shard_map/psum | solution.py:21
  235.8 0.0 all-reduce.7.cloned.1.call-update
  235.8 0.2 all-reduce.9.cloned.1.call-start
  236.1 7.7 %fusion = f32[256,4096]{1,0:T(8,128)} fusion(bf16[1024,4096]{1,0:T(8,128)(2,1)} %param.2, f32[1024,256]{1,0:T(8,128)S(1)} %fusion.17), kind=kOutput, calls=%fused_computation.5 | convolution fusion | flops 2147745792 | bytes 13631488 | tf_op jit(solution)/shard_map/dot_general | solution.py:15
  243.8 0.0 all-reduce.9.cloned.1.call-update
  243.8 0.6 iota_compare_fusion
  244.5 20.6 %all-reduce.7.cloned.1.call-done = f32[256,256]{0,1:T(8,128)} async-done(((f32[256,256]{0,1:T(8,128)}), f32[256,256]{0,1:T(8,128)}) %all-reduce.7.cloned.1.call-update) | async-done | bytes 262160 | tf_op jit(solution)/shard_map/psum | solution.py:21
  265.0 1.1 copy.6
  266.1 1.0 fusion.2
  267.1 0.0 copy-start.2
  267.1 0.7 copy-done.2
  267.8 11.7 %cholesky.50 = f32[128,128]{1,0:T(8,128)S(1)} custom-call(f32[128,128]{1,0:T(8,128)S(1)} %cholesky.118), custom_call_target="Cholesky" | custom-call | tf_op jit(solution)/shard_map/jit(cholesky)/cholesky | solution.py:22
  279.6 9.8 %custom-call.14 = f32[1,128,128]{1,2,0:T(8,128)S(1)} custom-call(f32[1,128,128]{2,1,0:T(8,128)S(1)} %get-tuple-element.29), custom_call_target="InvertDiagBlocksLowerTriangular" | custom-call | tf_op jit(solution)/shard_map/jit(cholesky)/cholesky | solution.py:22
  289.4 1.0 constant_dynamic-update-slice_fusion
  290.5 1.1 convolution_subtract_fusion.1
  291.6 11.9 %cholesky.105 = f32[128,128]{1,0:T(8,128)S(1)} custom-call(f32[128,128]{1,0:T(8,128)S(1)} %convolution_subtract_fusion.1), custom_call_target="Cholesky" | custom-call | tf_op jit(solution)/shard_map/jit(cholesky)/cholesky | solution.py:22
  303.5 0.0 copy-start.1
  303.5 0.6 compare_reduce_fusion
  305.3 0.0 copy-done.1
  305.3 1.7 multiply_bitcast_fusion
  307.0 0.1 triangular_solve.63
  307.1 5.0 while.1
  307.1 0.6 fusion.30
  307.7 1.9 bitcast_dynamic-update-slice_fusion.2
  309.6 0.6 fusion.30
  310.2 1.9 bitcast_dynamic-update-slice_fusion.2
  312.1 21.1 %custom-call.15 = f32[2,128,128]{1,2,0:T(8,128)} custom-call(f32[2,128,128]{2,1,0:T(8,128)} %get-tuple-element.10), custom_call_target="InvertDiagBlocksLowerTriangular" | custom-call | tf_op jit(solution)/shard_map/triangular_solve | solution.py:25
  333.2 1.8 copy.7
  335.0 1.1 fusion.6
  336.1 1.0 convolution_subtract_fusion
  337.2 1.1 fusion.9
  338.3 2.0 convolution_multiply_fusion
  340.3 202.3 %all-reduce.9.cloned.1.call-done = f32[256,4096]{1,0:T(8,128)} async-done(((f32[256,4096]{1,0:T(8,128)}), f32[256,4096]{1,0:T(8,128)}) %all-reduce.9.cloned.1.call-update) | async-done | bytes 4194320 | tf_op jit(solution)/shard_map/psum | solution.py:19
  542.6 1.9 fusion.4
  (8 shorter events, 0.1 us)
Async XLA Ops:
  7.2 1.6 copy-start
  7.2 228.6 %all-reduce.5.cloned.1.call-start = ((), (), s32[]{:S(2)}) async-start(), calls=%async_computation | async-start | bytes 524288 | tf_op jit(solution)/shard_map/psum | solution.py:21
  17.0 248.0 %all-reduce.7.cloned.1.call-start = ((), (), s32[]{:S(2)}) async-start(), calls=%async_computation.1 | async-start | bytes 524288 | tf_op jit(solution)/shard_map/psum | solution.py:21
  235.8 306.7 %all-reduce.9.cloned.1.call-start = ((), (), s32[]{:S(2)}) async-start(), calls=%async_computation.2 | async-start | bytes 8388608 | tf_op jit(solution)/shard_map/psum | solution.py:19
  267.1 0.7 copy-start.2
  303.5 1.9 copy-start.1
Sparse Core Ops, SparseCore 0:
  17.1 218.6 all-reduce.4
  238.4 26.5 all-reduce.6
  270.5 272.0 all-reduce.8
